TPU v7x, 32 devices: a whole 2x2x4 slice. The times are simulated.
32 devices in a mesh: expert: 4 (over y, core), shard: 8 (over z, x).
Axes of the slice: x: 2, y: 2, z: 4, core: 2. Of those that a mesh axis runs over, the one named last changes fastest.
Arguments:
- train_down: float32 [16, 6400, 4096], P('expert', None, 'shard'), may hold values from -0.109375 to 0.109375
- other_down: bfloat16 [16, 6400, 4096], P('expert', None, 'shard'), may hold values from -0.0390625 to 0.0390625
- router_weight: float32 [4096, 16], P('shard', 'expert'), may hold values from -0.09375 to 0.09375
- router_gain: float32 [4096], P('shard'), may hold values from 0.25 to 1.75
Outputs:
- ready_down: bfloat16 [16, 6400, 4096], P('expert', 'shard')
- scale_down: float32 [16, 6400], P('expert', 'shard')
- serve_router: bfloat16 [4096, 16], replicated
All inputs are finite; a program needn't handle non-finite values.
Results may differ from a plain program's by a relative error of at most 0.001.
Values may be sent and summed in bfloat16 or wider, within the bound.
A program may use at most 256 MiB of HBM per device.

v0:
```python
import jax
import jax.numpy as jnp
from jax import lax
from jax.sharding import PartitionSpec as P


def per_device(train_down, other_down, router_weight, router_gain):
    latest_down = train_down + other_down.astype(jnp.float32)
    total_down = lax.psum(jnp.sum(latest_down * latest_down, axis=2), "shard")
    scale_down = jnp.sqrt(total_down)
    narrow_down = (latest_down / jnp.expand_dims(scale_down, 2)).astype(jnp.bfloat16)
    ready_down = lax.all_to_all(narrow_down, "shard", split_axis=1, concat_axis=2, tiled=True)
    scale_down = lax.dynamic_slice_in_dim(
        scale_down, lax.axis_index("shard") * ready_down.shape[1], ready_down.shape[1], axis=1
    )
    part_router = (router_weight * router_gain[:, None]).astype(jnp.bfloat16)
    row_router = lax.all_gather(part_router, "shard", axis=0, tiled=True)
    serve_router = lax.all_gather(row_router, "expert", axis=1, tiled=True)
    return (ready_down, scale_down, serve_router)


def solution(mesh):
    in_specs = (
        P("expert", None, "shard"),
        P("expert", None, "shard"),
        P("shard", "expert"),
        P("shard"),
    )
    out_specs = (P("expert", "shard", None), P("expert", "shard"), P())
    return jax.shard_map(
        per_device, mesh=mesh, in_specs=in_specs, out_specs=out_specs, check_vma=False
    )
```

profile of v0, /device:TPU:0, one launch (start us, length us, event | category | flops | bytes accessed | tf_op | source)
XLA Modules:
  0.0 905.5 jit_solution(8188198296431997854)
XLA Ops:
  7.2 0.0 all-reduce.2.cloned.1.call-start
  7.2 24.2 %multiply_reduce_fusion = f32[4,6400]{1,0:T(4,128)S(1)} fusion(f32[4,6400,512]{2,1,0:T(8,128)} %param.4, bf16[4,6400,512]{2,1,0:T(8,128)(2,1)} %param.5), kind=kLoop, calls=%fused_computation.1 | loop fusion | flops 52403200 | bytes 78745600 | tf_op jit(solution)/shard_map/reduce_sum | solution.py:9
  31.4 2.3 copy.21
  33.7 0.0 all-reduce.2.cloned.1.call-update
  33.7 135.6 %all-reduce.2.cloned.1.call-done = f32[4,6400]{0,1:T(8,128)} async-done(((f32[4,6400]{0,1:T(8,128)}), f32[4,6400]{0,1:T(8,128)}) %all-reduce.2.cloned.1.call-update) | async-done | bytes 102416 | tf_op jit(solution)/shard_map/psum | solution.py:9
  169.3 2.7 sqrt.3
  172.0 1.2 copy.17
  173.3 34.3 %divide_convert_fusion = bf16[4,6400,512]{2,1,0:T(8,128)(2,1)} fusion(f32[4,6400,512]{2,1,0:T(8,128)} %param.4, bf16[4,6400,512]{2,1,0:T(8,128)(2,1)} %param.5, f32[4,6400]{1,0:T(4,128)S(1)} %copy.17), kind=kLoop, calls=%fused_computation | loop fusion | flops 52428800 | bytes 104960000 | tf_op jit(solution)/shard_map/convert_element_type | solution.py:11
  207.5 33.4 %copy.18 = bf16[4,6400,512]{2,0,1:T(4,128)(2,1)} copy(bf16[4,6400,512]{2,1,0:T(8,128)(2,1)} %divide_convert_fusion) | data formatting | bytes 52428800 | tf_op jit(solution)/shard_map/convert_element_type | solution.py:11
  240.9 0.0 copy-start
  240.9 0.0 copy-start.1
  240.9 6.6 all-to-all-start
  247.6 0.0 copy-done
  247.6 0.0 copy-done.1
  247.6 585.0 %all_gather.6 = bf16[4096,4]{0,1:T(4,128)(2,1)S(1)} all-gather(bf16[512,4]{0,1:T(4,128)(2,1)S(1)} %multiply_convert_fusion), channel_id=1, replica_groups=mesh['expert'=4,'shard'=8] {'shard'}, dimensions={0}, use_global_device_ids=true | all-gather | bytes 36864 | tf_op jit(solution)/shard_map/all_gather | solution.py:17
  832.7 5.4 all-gather
  838.1 0.7 reshape.9
  838.8 0.8 constant_dynamic-slice_fusion
  839.5 1.8 copy.20
  841.3 0.0 all-to-all-done
  841.3 18.2 %copy.19 = bf16[4,800,8,512]{3,2,1,0:T(8,128)(2,1)} copy(bf16[4,800,8,512]{3,0,1,2:T(4,128)(2,1)} %bitcast.1) | data formatting | bytes 52428800 | tf_op jit(solution)/shard_map/all_to_all | solution.py:12
  859.5 39.2 %all_to_all.16 = bf16[4,800,4096]{2,1,0:T(8,128)(2,1)} reshape(bf16[4,800,8,512]{3,2,1,0:T(8,128)(2,1)} %copy.19) | data formatting | bytes 52428800 | tf_op jit(solution)/shard_map/all_to_all | solution.py:12
  (1 shorter events, 0.0 us)
Async XLA Ops:
  7.2 162.2 %all-reduce.2.cloned.1.call-start = ((), (), s32[]{:S(2)}) async-start(), calls=%async_computation.1 | async-start | bytes 6553600 | tf_op jit(solution)/shard_map/psum | solution.py:9
  240.9 6.7 copy-start
  240.9 6.7 copy-start.1
  240.9 600.4 %all-to-all-start = ((bf16[4,6400,512]{2,0,1:T(4,128)(2,1)}), bf16[4,6400,512]{2,0,1:T(4,128)(2,1)}, u32[]{:S(2)}, u32[]{:S(2)}) async-start(bf16[4,6400,512]{2,0,1:T(4,128)(2,1)} %copy.18), calls=%async_computation | async-start | bytes 52428800 | tf_op jit(solution)/shard_map/all_to_all | solution.py:12
Sparse Core Ops, SparseCore 0:
  33.9 135.4 all-reduce.1
where the time goes:
time: 907 us; the launch traced here: 906 us
  blocking collectives  590 us (65%)
  waiting for transfers between devices  136 us (15%)
  local copies, waits for them, and re-layouts  100 us (11%)
  other arithmetic  58.5 us (6%)
  between operations  14.1 us (2%)
    all_gather x1, blocking collectives, per_device(): row_router = lax.all_gather(part_router, 'shard', axis=0, tiled=True)  585 us
    psum x1, waiting for transfers between devices, per_device(): total_down = lax.psum(jnp.sum(latest_down * latest_down, axis=2), 'shard')  136 us
    all_to_all x2, local copies, waits for them, and re-layouts, per_device(): lax.all_to_all(narrow_down, 'shard', split_axis=1, concat_axis=2, tiled=T...  57.4 us
    convert_element_type x1, other arithmetic, per_device(): (latest_down / jnp.expand_dims(scale_down, 2)).astype(jnp.bfloat16)  34.3 us
    convert_element_type x1, local copies, waits for them, and re-layouts, per_device(): (latest_down / jnp.expand_dims(scale_down, 2)).astype(jnp.bfloat16)  33.4 us
    reduce_sum x1, other arithmetic, per_device(): total_down = lax.psum(jnp.sum(latest_down * latest_down, axis=2), 'shard')  24.2 us
  transfers between devices with their start and end apart: 2, of which 1 were waited for; matrix products, arithmetic and copies ran while one was open for 0% of the time, Pallas kernels for 0%

commit v1 on v0

--- a/solution.py
+++ b/solution.py
@@ -15,7 +15,7 @@
     )
     part_router = (router_weight * router_gain[:, None]).astype(jnp.bfloat16)
     row_router = lax.all_gather(part_router, "shard", axis=0, tiled=True)
-    serve_router = lax.all_gather(row_router, "expert", axis=1, tiled=True)
+    serve_router = jnp.concatenate(lax.all_gather(row_router, "expert"), axis=1)
     return (ready_down, scale_down, serve_router)
 
 

time: 907 us -> 907 us (level)
  no operation moved by 1% of the time
where the time goes in v1:
time: 907 us; the launch traced here: 906 us
  blocking collectives  590 us (65%)
  waiting for transfers between devices  136 us (15%)
  local copies, waits for them, and re-layouts  100 us (11%)
  other arithmetic  58.5 us (6%)
  between operations  14.1 us (2%)
    all_gather x1, blocking collectives, per_device(): row_router = lax.all_gather(part_router, 'shard', axis=0, tiled=True)  585 us
    psum x1, waiting for transfers between devices, per_device(): total_down = lax.psum(jnp.sum(latest_down * latest_down, axis=2), 'shard')  136 us
    all_to_all x2, local copies, waits for them, and re-layouts, per_device(): lax.all_to_all(narrow_down, 'shard', split_axis=1, concat_axis=2, tiled=T...  57.4 us
    convert_element_type x1, other arithmetic, per_device(): (latest_down / jnp.expand_dims(scale_down, 2)).astype(jnp.bfloat16)  34.3 us
    convert_element_type x1, local copies, waits for them, and re-layouts, per_device(): (latest_down / jnp.expand_dims(scale_down, 2)).astype(jnp.bfloat16)  33.4 us
    reduce_sum x1, other arithmetic, per_device(): total_down = lax.psum(jnp.sum(latest_down * latest_down, axis=2), 'shard')  24.2 us
  transfers between devices with their start and end apart: 2, of which 1 were waited for; matrix products, arithmetic and copies ran while one was open for 0% of the time, Pallas kernels for 0%

profile of v1, /device:TPU:0, one launch (start us, length us, event | category | flops | bytes accessed | tf_op | source)
XLA Modules:
  0.0 905.5 jit_solution(448214093036344014)
XLA Ops:
  7.2 0.0 all-reduce.2.cloned.1.call-start
  7.2 24.2 %multiply_reduce_fusion = f32[4,6400]{1,0:T(4,128)S(1)} fusion(f32[4,6400,512]{2,1,0:T(8,128)} %param.4, bf16[4,6400,512]{2,1,0:T(8,128)(2,1)} %param.5), kind=kLoop, calls=%fused_computation.1 | loop fusion | flops 52403200 | bytes 78745600 | tf_op jit(solution)/shard_map/reduce_sum | solution.py:9
  31.4 2.3 copy.25
  33.7 0.0 all-reduce.2.cloned.1.call-update
  33.7 135.6 %all-reduce.2.cloned.1.call-done = f32[4,6400]{0,1:T(8,128)} async-done(((f32[4,6400]{0,1:T(8,128)}), f32[4,6400]{0,1:T(8,128)}) %all-reduce.2.cloned.1.call-update) | async-done | bytes 102416 | tf_op jit(solution)/shard_map/psum | solution.py:9
  169.3 2.7 sqrt.3
  172.0 1.2 copy.20
  173.3 34.3 %divide_convert_fusion = bf16[4,6400,512]{2,1,0:T(8,128)(2,1)} fusion(f32[4,6400,512]{2,1,0:T(8,128)} %param.4, bf16[4,6400,512]{2,1,0:T(8,128)(2,1)} %param.5, f32[4,6400]{1,0:T(4,128)S(1)} %copy.20), kind=kLoop, calls=%fused_computation | loop fusion | flops 52428800 | bytes 104960000 | tf_op jit(solution)/shard_map/convert_element_type | solution.py:11
  207.5 33.4 %copy.21 = bf16[4,6400,512]{2,0,1:T(4,128)(2,1)} copy(bf16[4,6400,512]{2,1,0:T(8,128)(2,1)} %divide_convert_fusion) | data formatting | bytes 52428800 | tf_op jit(solution)/shard_map/convert_element_type | solution.py:11
  240.9 0.0 copy-start
  240.9 0.0 copy-start.1
  240.9 6.6 all-to-all-start
  247.6 0.0 copy-done
  247.6 0.0 copy-done.1
  247.6 585.0 %all_gather.9 = bf16[4096,4]{0,1:T(4,128)(2,1)S(1)} all-gather(bf16[512,4]{0,1:T(4,128)(2,1)S(1)} %multiply_convert_fusion), channel_id=1, replica_groups=mesh['expert'=4,'shard'=8] {'shard'}, dimensions={0}, use_global_device_ids=true | all-gather | bytes 36864 | tf_op jit(solution)/shard_map/all_gather | solution.py:17
  832.7 5.4 all-gather
  838.1 0.7 reshape.15
  838.8 0.8 constant_dynamic-slice_fusion
  839.5 1.8 copy.24
  841.3 0.0 all-to-all-done
  841.3 18.2 %copy.22 = bf16[4,800,8,512]{3,2,1,0:T(8,128)(2,1)} copy(bf16[4,800,8,512]{3,0,1,2:T(4,128)(2,1)} %bitcast.1) | data formatting | bytes 52428800 | tf_op jit(solution)/shard_map/all_to_all | solution.py:12
  859.5 39.2 %all_to_all.16 = bf16[4,800,4096]{2,1,0:T(8,128)(2,1)} reshape(bf16[4,800,8,512]{3,2,1,0:T(8,128)(2,1)} %copy.22) | data formatting | bytes 52428800 | tf_op jit(solution)/shard_map/all_to_all | solution.py:12
  (1 shorter events, 0.0 us)
Async XLA Ops:
  7.2 162.2 %all-reduce.2.cloned.1.call-start = ((), (), s32[]{:S(2)}) async-start(), calls=%async_computation.1 | async-start | bytes 6553600 | tf_op jit(solution)/shard_map/psum | solution.py:9
  240.9 6.7 copy-start
  240.9 6.7 copy-start.1
  240.9 600.4 %all-to-all-start = ((bf16[4,6400,512]{2,0,1:T(4,128)(2,1)}), bf16[4,6400,512]{2,0,1:T(4,128)(2,1)}, u32[]{:S(2)}, u32[]{:S(2)}) async-start(bf16[4,6400,512]{2,0,1:T(4,128)(2,1)} %copy.21), calls=%async_computation | async-start | bytes 52428800 | tf_op jit(solution)/shard_map/all_to_all | solution.py:12
Sparse Core Ops, SparseCore 0:
  33.9 135.4 all-reduce.1

commit v2 on v0

--- a/solution.py
+++ b/solution.py
@@ -6,7 +6,9 @@
 
 def per_device(train_down, other_down, router_weight, router_gain):
     latest_down = train_down + other_down.astype(jnp.float32)
-    total_down = lax.psum(jnp.sum(latest_down * latest_down, axis=2), "shard")
+    total_down = jnp.sum(
+        lax.all_gather(jnp.sum(latest_down * latest_down, axis=2), "shard"), axis=0
+    )
     scale_down = jnp.sqrt(total_down)
     narrow_down = (latest_down / jnp.expand_dims(scale_down, 2)).astype(jnp.bfloat16)
     ready_down = lax.all_to_all(narrow_down, "shard", split_axis=1, concat_axis=2, tiled=True)

time: 907 us -> 781 us (0.86)
  waiting for transfers between devices: 136 us -> 0.01 us
  blocking collectives: 590 us -> 620 us
  between operations: 14.1 us -> 0.71 us
    psum x1 -> x0, waiting for transfers between devices: 136 us -> none  [per_device(): total_down = lax.psum(jnp.sum(latest_down * latest_down, axis=2), 'shard')]
    all_gather x0 -> x1, blocking collectives: none -> 33.9 us  [per_device(): lax.all_gather(jnp.sum(latest_down * latest_down, axis=2), 'shard')]
    reduce_sum x1 -> x2, other arithmetic: 24.2 us -> 24.4 us  [the longest x1 24.2 us: per_device(): jnp.sum(latest_down * latest_down, axis=2)]
  transfers between devices with their start and end apart: 2 -> 1, of which waited for: 1 -> 0; matrix products, arithmetic and copies ran while one was open for 0% -> 0% of each run, Pallas kernels for 0% -> 0%
where the time goes in v2:
time: 781 us; the launch traced here: 780 us
  blocking collectives  620 us (79%)
  local copies, waits for them, and re-layouts  94.5 us (12%)
  other arithmetic  58.7 us (8%)
    all_gather x1, blocking collectives, per_device(): row_router = lax.all_gather(part_router, 'shard', axis=0, tiled=True)  580 us
    all_to_all x2, local copies, waits for them, and re-layouts, per_device(): lax.all_to_all(narrow_down, 'shard', split_axis=1, concat_axis=2, tiled=T...  57.4 us
    convert_element_type x1, other arithmetic, per_device(): (latest_down / jnp.expand_dims(scale_down, 2)).astype(jnp.bfloat16)  34.3 us
    all_gather x1, blocking collectives, per_device(): lax.all_gather(jnp.sum(latest_down * latest_down, axis=2), 'shard')  33.9 us
    convert_element_type x1, local copies, waits for them, and re-layouts, per_device(): (latest_down / jnp.expand_dims(scale_down, 2)).astype(jnp.bfloat16)  33.4 us
    reduce_sum x1, other arithmetic, per_device(): jnp.sum(latest_down * latest_down, axis=2)  24.2 us
  transfers between devices with their start and end apart: 1, of which 0 were waited for; matrix products, arithmetic and copies ran while one was open for 0% of the time, Pallas kernels for 0%

profile of v2, /device:TPU:0, one launch (start us, length us, event | category | flops | bytes accessed | tf_op | source)
XLA Modules:
  0.0 780.0 jit_solution(1847130021066882002)
XLA Ops:
  0.6 24.2 %multiply_reduce_fusion = f32[4,6400]{1,0:T(4,128)S(1)} fusion(f32[4,6400,512]{2,1,0:T(8,128)} %param.4, bf16[4,6400,512]{2,1,0:T(8,128)(2,1)} %param.5), kind=kLoop, calls=%fused_computation.1 | loop fusion | flops 52403200 | bytes 78745600 | tf_op jit(solution)/shard_map/reduce_sum | solution.py:10
  24.9 1.1 copy.21
  26.0 1.2 copy.18
  27.2 33.9 %all-gather.1 = f32[8,4,6400]{2,1,0:T(4,128)S(1)} all-gather(f32[1,4,6400]{2,1,0:T(4,128)S(1)} %copy.18), channel_id=2, replica_groups=mesh['expert'=4,'shard'=8] {'shard'}, dimensions={0}, use_global_device_ids=true | all-gather | bytes 921600 | tf_op jit(solution)/shard_map/all_gather | solution.py:10
  61.2 0.1 reduce_sum.19
  61.3 0.1 sqrt.7
  61.4 34.3 %divide_convert_fusion = bf16[4,6400,512]{2,1,0:T(8,128)(2,1)} fusion(f32[4,6400,512]{2,1,0:T(8,128)} %param.4, bf16[4,6400,512]{2,1,0:T(8,128)(2,1)} %param.5, f32[4,6400]{1,0:T(4,128)S(1)} %sqrt.7), kind=kLoop, calls=%fused_computation | loop fusion | flops 52428800 | bytes 104960000 | tf_op jit(solution)/shard_map/convert_element_type | solution.py:13
  95.6 0.0 copy-start
  95.6 0.0 copy-start.1
  95.7 33.4 %copy.19 = bf16[4,6400,512]{2,0,1:T(4,128)(2,1)} copy(bf16[4,6400,512]{2,1,0:T(8,128)(2,1)} %divide_convert_fusion) | data formatting | bytes 52428800 | tf_op jit(solution)/shard_map/convert_element_type | solution.py:13
  129.0 6.5 all-to-all-start
  135.5 0.0 copy-done
  135.6 0.0 copy-done.1
  135.6 580.2 %all_gather.14 = bf16[4096,4]{0,1:T(4,128)(2,1)S(1)} all-gather(bf16[512,4]{0,1:T(4,128)(2,1)S(1)} %multiply_convert_fusion), channel_id=1, replica_groups=mesh['expert'=4,'shard'=8] {'shard'}, dimensions={0}, use_global_device_ids=true | all-gather | bytes 36864 | tf_op jit(solution)/shard_map/all_gather | solution.py:19
  715.8 5.4 all-gather.2
  721.2 0.7 reshape.14
  721.9 0.7 constant_dynamic-slice_fusion
  722.6 0.0 all-to-all-done
  722.6 18.2 %copy.20 = bf16[4,800,8,512]{3,2,1,0:T(8,128)(2,1)} copy(bf16[4,800,8,512]{3,0,1,2:T(4,128)(2,1)} %bitcast.2) | data formatting | bytes 52428800 | tf_op jit(solution)/shard_map/all_to_all | solution.py:14
  740.8 39.2 %all_to_all.16 = bf16[4,800,4096]{2,1,0:T(8,128)(2,1)} reshape(bf16[4,800,8,512]{3,2,1,0:T(8,128)(2,1)} %copy.20) | data formatting | bytes 52428800 | tf_op jit(solution)/shard_map/all_to_all | solution.py:14
  (1 shorter events, 0.0 us)
Async XLA Ops:
  95.6 39.9 %copy-start = (f32[512,4]{0,1:T(4,128)S(1)}, f32[512,4]{0,1:T(4,128)}, u32[]{:S(2)}) copy-start(f32[512,4]{0,1:T(4,128)} %param.6) | copy-start | bytes 24580
  95.6 39.9 %copy-start.1 = (f32[512]{0:T(512)S(1)}, f32[512]{0:T(512)}, u32[]{:S(2)}) copy-start(f32[512]{0:T(512)} %param.7) | copy-start | bytes 6148
  129.0 593.6 %all-to-all-start = ((bf16[4,6400,512]{2,0,1:T(4,128)(2,1)}), bf16[4,6400,512]{2,0,1:T(4,128)(2,1)}, u32[]{:S(2)}, u32[]{:S(2)}) async-start(bf16[4,6400,512]{2,0,1:T(4,128)(2,1)} %copy.19), calls=%async_computation | async-start | bytes 52428800 | tf_op jit(solution)/shard_map/all_to_all | solution.py:14
